TPU v7x, 128 devices: a whole 4x4x4 slice. The times are simulated.
128 devices in a mesh: row: 8 (over x_hi, z), col: 16 (over x_lo, y, core).
Axes of the slice: x: 4 (x_hi: 2, x_lo: 2; x = x_hi * 2 + x_lo), y: 4, z: 4, core: 2. Of those that a mesh axis runs over, the one named last changes fastest.
Arguments:
- customer_inputs: bfloat16 [131072, 1024], P(('row', 'col')), may hold values from -6 to 6
- candidate_inputs: bfloat16 [131072, 1024], P(('row', 'col')), may hold values from -6 to 6
- affinity_sharpness: bfloat16 [131072], P(('row', 'col')), may hold values from 4 to 40
- correct_candidate_index: int32 [131072], P(('row', 'col')), may hold values from 0 to 8191
- customer_initial_weights: bfloat16 [1024, 512], replicated, may hold values from -0.1875 to 0.1875
- customer_final_weights: bfloat16 [512, 256], replicated, may hold values from -0.25 to 0.25
- candidate_initial_weights: bfloat16 [1024, 512], replicated, may hold values from -0.1875 to 0.1875
- candidate_final_weights: bfloat16 [512, 256], replicated, may hold values from -0.25 to 0.25
Outputs:
- loss: float32 [], replicated
- grad_user_first: float32 [1024, 512], replicated
- grad_user_second: float32 [512, 256], replicated
- grad_item_first: float32 [1024, 512], replicated
- grad_item_second: float32 [512, 256], replicated
Inputs may be any that keep to these rules, and one draw needn't show every extreme that they name: correct_candidate_index[u] indexes the items of u's group in the order of the steps.
All inputs are finite; a program needn't handle non-finite values.
Results may differ from a plain program's by a relative error of at most 0.015.
Values may be sent and summed in bfloat16 or wider, within the bound.
No kernel may reach another device: no remote copies, remote signals or barrier semaphores. Data moves between devices by JAX's collectives and lax.ppermute only.
A program may use at most 128 MiB of HBM per device.

v0:
```python
import jax
import jax.numpy as jnp
from jax import lax
from jax.sharding import PartitionSpec as P

EPS = 1e-06


def laid_out(tiles, dim):
    dims = list(tiles.shape[1:])
    dims[dim] *= tiles.shape[0]
    return jnp.moveaxis(tiles, 0, dim).reshape(dims)


def copy_for_each(value, axis):
    copies = jnp.broadcast_to(value, (lax.axis_size(axis), *value.shape))
    return lax.all_to_all(copies, axis, split_axis=0, concat_axis=0, tiled=True)


def gathered_copies(value, axis, dim):
    return laid_out(copy_for_each(value, axis), dim)


def tower_forward(feats, first, second):
    pre = jnp.dot(feats, first, preferred_element_type=jnp.float32)
    hidden = jax.nn.relu(pre).astype(jnp.bfloat16)
    out = jnp.dot(hidden, second, preferred_element_type=jnp.float32)
    inv = lax.rsqrt(jnp.mean(out * out, axis=-1, keepdims=True) + EPS)
    return ((out * inv).astype(jnp.bfloat16), (pre, hidden, out, inv))


def tower_backward(feats, second, saved, grad_vec):
    pre, hidden, out, inv = saved
    grad = grad_vec.astype(jnp.float32)
    normed = out * inv
    grad_out = (inv * (grad - normed * jnp.mean(grad * normed, axis=-1, keepdims=True))).astype(
        jnp.bfloat16
    )
    grad_second = jnp.dot(hidden.T, grad_out, preferred_element_type=jnp.float32)
    grad_hidden = jnp.dot(grad_out, second.T, preferred_element_type=jnp.float32)
    grad_pre = jnp.where(pre > 0, grad_hidden, 0.0).astype(jnp.bfloat16)
    grad_first = jnp.dot(feats.T, grad_pre, preferred_element_type=jnp.float32)
    return (grad_first, grad_second)


def positive_pair_logit(
    shopper_vector, gathered_entries, affinity_sharpness, correct_candidate_index, resident_table
):
    latent_code = shopper_vector.shape[-1]
    coolness_fp32_number = affinity_sharpness.astype(jnp.float32)
    affinity_matrix = (
        coolness_fp32_number[:, None]
        * jnp.einsum(
            "ue,ie->ui", shopper_vector, gathered_entries, preferred_element_type=jnp.float32
        )
        / latent_code
    )
    lse = jax.nn.logsumexp(affinity_matrix, axis=1)
    columns = lax.broadcasted_iota(jnp.int32, affinity_matrix.shape, 1)
    target_column = columns == correct_candidate_index[:, None]
    picked = jnp.sum(jnp.where(target_column, affinity_matrix, 0.0), axis=1)
    softmax_likelihood = jnp.exp(affinity_matrix - lse[:, None])
    sensitivity_of_affinities = (
        (softmax_likelihood - target_column.astype(jnp.float32))
        * (coolness_fp32_number / (latent_code * resident_table))[:, None]
    ).astype(jnp.bfloat16)
    customer_derivative = jnp.dot(
        sensitivity_of_affinities, gathered_entries, preferred_element_type=jnp.float32
    )
    return (lse, sensitivity_of_affinities, customer_derivative, jnp.sum(lse - picked))


def body(
    customer_inputs,
    candidate_inputs,
    affinity_sharpness,
    correct_candidate_index,
    customer_initial_weights,
    customer_final_weights,
    candidate_initial_weights,
    candidate_final_weights,
):
    resident_table = customer_inputs.shape[0]
    shopper_vector, user_saved = tower_forward(
        customer_inputs, customer_initial_weights, customer_final_weights
    )
    offered_thing_vector, item_saved = tower_forward(
        candidate_inputs, candidate_initial_weights, candidate_final_weights
    )
    latent_code = shopper_vector.shape[-1]
    gathered_entries = lax.all_gather(offered_thing_vector, "row", axis=0, tiled=True)
    lse, sensitivity_of_affinities, customer_derivative, loss_local = positive_pair_logit(
        shopper_vector,
        gathered_entries,
        affinity_sharpness,
        correct_candidate_index,
        resident_table,
    )
    all_users, all_scales = (
        lax.all_gather(shopper_vector, "row", axis=0, tiled=True),
        lax.all_gather(affinity_sharpness, "row", axis=0, tiled=True),
    )
    all_positive = gathered_copies(correct_candidate_index, "row", 0)
    all_lse = gathered_copies(lse, "row", 0)
    coolness_fp32_number = all_scales.astype(jnp.float32)
    affinity_matrix = (
        coolness_fp32_number[:, None]
        * jnp.einsum(
            "ue,ie->ui", all_users, offered_thing_vector, preferred_element_type=jnp.float32
        )
        / latent_code
    )
    start = lax.axis_index("row") * resident_table
    columns = lax.broadcasted_iota(jnp.int32, affinity_matrix.shape, 1) + start
    target_column = columns == all_positive[:, None]
    softmax_likelihood = jnp.exp(affinity_matrix - all_lse[:, None])
    group_dlogits = (
        (softmax_likelihood - target_column.astype(jnp.float32))
        * (coolness_fp32_number / (latent_code * resident_table))[:, None]
    ).astype(jnp.bfloat16)
    candidate_derivative = jnp.einsum(
        "ui,ue->ie", group_dlogits, all_users, preferred_element_type=jnp.float32
    )
    grad_user_first, grad_user_second = tower_backward(
        customer_inputs,
        customer_final_weights,
        user_saved,
        customer_derivative.astype(jnp.bfloat16),
    )
    grad_item_first, grad_item_second = tower_backward(
        candidate_inputs,
        candidate_final_weights,
        item_saved,
        candidate_derivative.astype(jnp.bfloat16),
    )
    summed = (
        lax.psum(grad_user_first.astype(jnp.bfloat16), ("row", "col")).astype(jnp.float32),
        lax.psum(grad_user_second.astype(jnp.bfloat16), ("row", "col")).astype(jnp.float32),
        lax.psum(grad_item_first.astype(jnp.bfloat16), ("row", "col")).astype(jnp.float32),
        lax.psum(grad_item_second.astype(jnp.bfloat16), ("row", "col")).astype(jnp.float32),
        lax.psum(loss_local.astype(jnp.bfloat16), ("row", "col")).astype(jnp.float32),
    )
    users_total = resident_table * lax.axis_size("row") * lax.axis_size("col")
    return (summed[4] / users_total, summed[0], summed[1], summed[2], summed[3])


def solution(mesh):
    placed = (
        P(("row", "col"), None),
        P(("row", "col"), None),
        P(("row", "col")),
        P(("row", "col")),
        P(),
        P(),
        P(),
        P(),
    )
    return jax.shard_map(
        body, mesh=mesh, in_specs=placed, out_specs=(P(), P(), P(), P(), P()), check_vma=False
    )
```

profile of v0, /device:TPU:1, one launch (start us, length us, event | category | flops | bytes accessed | tf_op | source)
XLA Modules:
  0.0 351.3 jit_solution(15818196188370760790)
XLA Ops:
  7.2 0.0 copy-start
  7.2 0.0 copy-start.11
  7.2 0.0 all-gather.3.cloned.1.call-start
  7.2 3.3 fusion.28
  10.5 0.0 copy-start.4
  10.5 1.3 copy-done.4
  11.8 0.0 copy-done.11
  11.8 0.0 copy-start.14
  11.8 0.5 multiply_reduce_fusion
  12.4 0.9 multiply_convert_fusion.8
  13.3 0.0 all-gather.3.cloned.1.call-update
  13.3 0.0 copy-done.14
  13.3 0.6 broadcast_in_dim.15
  13.9 8.3 %all-to-all-start.1 = ((s32[8,1,1024]{2,1,0:T(1,128)}), s32[8,1,1024]{2,1,0:T(1,128)S(1)}, u32[]{:S(2)}, u32[]{:S(2)}) async-start(s32[8,1,1024]{2,1,0:T(1,128)} %broadcast_in_dim.15), calls=%async_computation.1 | async-start | bytes 65536 | tf_op jit(solution)/shard_map/all_to_all | solution.py:17
  22.2 0.0 all-gather.5.cloned.1.call-start
  22.3 0.0 copy-done
  22.3 2.5 fusion.27
  24.8 0.0 copy-start.6
  24.8 1.3 copy-done.6
  26.1 0.0 copy-done.10
  26.1 0.5 multiply_reduce_fusion.1
  26.6 0.0 copy-start.2
  26.7 0.9 copy-done.2
  27.6 0.9 multiply_convert_fusion.9
  28.5 0.0 all-gather.5.cloned.1.call-update
  28.5 0.0 copy-done.13
  28.6 26.5 %all_gather.10 = bf16[8192]{0:T(1024)(128)(2,1)S(1)} all-gather(bf16[1024]{0:T(1024)(128)(2,1)S(1)} %copy-done.13), channel_id=1, replica_groups=mesh['row'=8,'col'=16] {'row'}, dimensions={0}, use_global_device_ids=true | all-gather | bytes 18432 | tf_op jit(solution)/shard_map/all_gather | solution.py:101
  55.1 32.1 %all-gather.3.cloned.1.call-done = bf16[8192,256]{0,1:T(8,128)(2,1)} async-done(((bf16[1024,256]{0,1:T(8,128)(2,1)}), bf16[8192,256]{0,1:T(8,128)(2,1)}) %all-gather.3.cloned.1.call-update) | async-done | bytes 4194320 | tf_op jit(solution)/shard_map/all_gather | solution.py:91
  87.2 16.0 %fusion = (f32[1024]{0:T(1024)S(1)}, f32[1024,8192]{1,0:T(8,128)}) fusion(f32[1024]{0:T(1024)S(1)} %convert_element_type.90, bf16[1024,256]{0,1:T(8,128)(2,1)} %multiply_convert_fusion.9, bf16[8192,256]{0,1:T(8,128)(2,1)} %all-gather.3.cloned.1.call-done), kind=kOutput, calls=%fused_computation.6 | convolution fusion | flops 4320132096 | bytes 38281216 | tf_op jit(solution)/shard_map/ue,ie->ui/dot_general | solution.py:53
  103.2 18.4 %select_reduce_fusion = (f32[1024]{0:T(1024)S(1)}, f32[1024]{0:T(1024)S(1)}) fusion(f32[1024,8192]{1,0:T(8,128)} %get-tuple-element.28, s32[1024]{0:T(1024)S(1)} %copy-done.14, f32[1024]{0:T(1024)S(1)} %convert_element_type.90, f32[1024]{0:T(1024)S(1)} %is-finite_select_fusion), kind=kLoop, calls=%fused_computation.2 | loop fusion | flops 58718208 | bytes 33574912 | tf_op jit(solution)/shard_map/reduce_sum | solution.py:61
  121.6 0.6 subtract_reduce_fusion
  122.2 0.0 copy-done.3
  122.3 20.4 %fusion.9 = (f32[1024]{0:T(1024)S(1)}, bf16[1024,256]{0,1:T(8,128)(2,1)S(1)}) fusion(f32[1024,256]{0,1:T(8,128)S(1)} %copy-done.3, f32[1024]{0:T(1024)S(1)} %add_rsqrt_fusion.1, bf16[8192,256]{0,1:T(8,128)(2,1)} %all-gather.3.cloned.1.call-done, f32[1024,8192]{1,0:T(8,128)} %get-tuple-element.28, f32[1024]{0:T(1024)S(1)} %broadcast_multiply_fusion.1, ...), kind=kOutput, calls=%fused_computation.26 | convolution fusion | flops 4363385856 | bytes 39346176 | tf_op jit(solution)/shard_map/dot_general | solution.py:67
  142.6 1.0 fusion.11
  143.6 4.4 %fusion.5 = bf16[1024,512]{0,1:T(8,128)(2,1)} fusion(bf16[1024,1024]{1,0:T(8,128)(2,1)S(1)} %copy-done, f32[1024,512]{1,0:T(8,128)} %copy-done.6, bf16[1024,256]{0,1:T(8,128)(2,1)} %fusion.11, bf16[512,256]{1,0:T(8,128)(2,1)S(1)} %copy-done.10), kind=kOutput, calls=%fused_computation.16 | convolution fusion | flops 1344274432 | bytes 6029312 | tf_op jit(solution)/shard_map/dot_general | solution.py:42
  148.0 0.0 all-to-all-done.1
  148.0 0.6 broadcast_in_dim.14
  148.6 3.3 all-to-all-start
  152.0 0.0 all-reduce.3.cloned.1.call-start
  152.0 2.9 convolution_convert_fusion.3
  154.9 4.5 %all-gather.5.cloned.1.call-done = bf16[8192,256]{0,1:T(8,128)(2,1)} async-done(((bf16[1024,256]{0,1:T(8,128)(2,1)}), bf16[8192,256]{0,1:T(8,128)(2,1)}) %all-gather.5.cloned.1.call-update) | async-done | bytes 4194320 | tf_op jit(solution)/shard_map/all_gather | solution.py:100
  159.4 0.0 all-to-all-done
  159.4 14.2 %multiply_convert_fusion.5.clone.4 = bf16[8192,1024]{1,0:T(8,128)(2,1)S(1)} fusion(f32[8192]{0:T(1024)S(1)} %broadcast_multiply_fusion, s32[1024]{0:T(1024)S(1)} %iota_add_fusion, f32[8192]{0:T(1024)S(1)} %bitcast.31, f32[8192]{0:T(1024)S(1)} %convert_element_type.108, s32[8192]{0:T(1024)S(1)} %bitcast.30, ...), kind=kOutput, calls=%fused_computation.clone.clone.clone.clone.clone.clone.1 | convolution fusion | flops 4362600448 | bytes 22159360 | tf_op jit(solution)/shard_map/ue,ie->ui/dot_general | solution.py:108
  173.6 0.0 copy-done.15
  173.6 0.0 copy-start.5
  173.6 0.0 copy-start.12
  173.7 4.7 %fusion.12 = (f32[1024]{0:T(1024)S(1)}, bf16[1024,256]{0,1:T(8,128)(2,1)S(1)}) fusion(f32[1024,256]{0,1:T(8,128)S(1)} %get-tuple-element.26, f32[1024]{0:T(1024)S(1)} %add_rsqrt_fusion, bf16[8192,256]{0,1:T(8,128)(2,1)S(1)} %copy-done.15, bf16[8192,1024]{1,0:T(8,128)(2,1)S(1)} %multiply_convert_fusion.5.clone.4), kind=kOutput, calls=%fused_computation.29 | convolution fusion | flops 4296276992 | bytes 22552576 | tf_op jit(solution)/shard_map/ui,ue->ie/dot_general | solution.py:121
  178.3 1.0 fusion.14
  179.3 0.0 copy-done.5
  179.3 0.0 copy-done.12
  179.3 4.4 %fusion.6 = bf16[1024,512]{0,1:T(8,128)(2,1)} fusion(bf16[1024,1024]{1,0:T(8,128)(2,1)} %param.9, f32[1024,512]{1,0:T(8,128)S(1)} %copy-done.5, bf16[1024,256]{0,1:T(8,128)(2,1)} %fusion.14, bf16[512,256]{1,0:T(8,128)(2,1)S(1)} %copy-done.12), kind=kOutput, calls=%fused_computation.17 | convolution fusion | flops 1344274432 | bytes 6029312 | tf_op jit(solution)/shard_map/dot_general | solution.py:42
  183.7 0.0 copy-done.7
  183.7 1.2 convolution_convert_fusion.2
  184.9 0.0 all-reduce.3.cloned.1.call-update
  185.0 0.0 copy-start.1
  185.0 64.6 %psum.35 = bf16[]{:T(256)} all-reduce(bf16[]{:T(256)} %get-tuple-element.21), channel_id=1, replica_groups=mesh['row'=8,'col'=16] {'row','col'}, use_global_device_ids=true, to_apply=%region_6.7 | all-reduce | flops 1 | bytes 4 | tf_op jit(solution)/shard_map/psum | solution.py:141
  250.2 86.5 %all-reduce.3.cloned.1.call-done = (bf16[1024,512]{0,1:T(8,128)(2,1)}, bf16[1024,512]{0,1:T(8,128)(2,1)}, bf16[512,256]{1,0:T(8,128)(2,1)}, bf16[512,256]{1,0:T(8,128)(2,1)}) async-done(((bf16[1024,512]{0,1:T(8,128)(2,1)}, bf16[1024,512]{0,1:T(8,128)(2,1)}, bf16[512,256]{1,0:T(8,128)(2,1)}, bf16[512,256]{1,0:T(8,128)(2,1)}), (bf16[1024,512]{0,1:T(8,128)(2,1)}, bf16[1024,512]{0,1:T(8,128)(2,1)}, ...) | async-done | bytes 2621456 | tf_op jit(solution)/shard_map/psum | solution.py:137
  336.8 2.7 copy.15
  339.5 1.8 convert_element_type.107
  341.2 0.0 copy-done.8
  341.2 1.6 copy.16
  342.8 0.0 copy-done.9
  342.8 0.8 convert_element_type.119
  343.7 0.0 copy-done.1
  (17 shorter events, 0.1 us)
Async XLA Ops:
  7.2 15.1 %copy-start = (bf16[1024,1024]{1,0:T(8,128)(2,1)S(1)}, bf16[1024,1024]{1,0:T(8,128)(2,1)}, u32[]{:S(2)}) copy-start(bf16[1024,1024]{1,0:T(8,128)(2,1)} %param.8) | copy-start | bytes 6291460
  7.2 4.7 %copy-start.11 = (bf16[512,256]{1,0:T(8,128)(2,1)S(1)}, bf16[512,256]{1,0:T(8,128)(2,1)}, u32[]{:S(2)}) copy-start(bf16[512,256]{1,0:T(8,128)(2,1)} %param.15) | copy-start | bytes 786436
  7.2 80.0 %all-gather.3.cloned.1.call-start = ((), (), s32[]{:S(2)}) async-start(), calls=%async_computation.2 | async-start | bytes 4718592 | tf_op jit(solution)/shard_map/all_gather | solution.py:91
  10.5 1.3 copy-start.4
  11.8 1.4 copy-start.14
  13.9 134.1 %all-to-all-start.1 = ((s32[8,1,1024]{2,1,0:T(1,128)}), s32[8,1,1024]{2,1,0:T(1,128)S(1)}, u32[]{:S(2)}, u32[]{:S(2)}) async-start(s32[8,1,1024]{2,1,0:T(1,128)} %broadcast_in_dim.15), calls=%async_computation.1 | async-start | bytes 65536 | tf_op jit(solution)/shard_map/all_to_all | solution.py:17
  22.2 3.9 %copy-start.10 = (bf16[512,256]{1,0:T(8,128)(2,1)S(1)}, bf16[512,256]{1,0:T(8,128)(2,1)}, u32[]{:S(2)}) copy-start(bf16[512,256]{1,0:T(8,128)(2,1)} %param.13) | copy-start | bytes 786436
  22.2 137.2 %all-gather.5.cloned.1.call-start = ((), (), s32[]{:S(2)}) async-start(), calls=%async_computation.3 | async-start | bytes 4718592 | tf_op jit(solution)/shard_map/all_gather | solution.py:100
  24.8 1.3 copy-start.6
  26.1 2.4 copy-start.13
  26.6 1.0 copy-start.2
  103.2 19.0 %copy-start.3 = (f32[1024,256]{0,1:T(8,128)S(1)}, f32[1024,256]{0,1:T(8,128)}, u32[]{:S(2)}) copy-start(f32[1024,256]{0,1:T(8,128)} %copy-done.2) | copy-start | bytes 3145732
  148.6 10.8 %all-to-all-start = ((f32[8,1,1024]{2,1,0:T(1,128)}), f32[8,1,1024]{2,1,0:T(1,128)S(1)}, u32[]{:S(2)}, u32[]{:S(2)}) async-start(f32[8,1,1024]{2,1,0:T(1,128)} %broadcast_in_dim.14), calls=%async_computation | async-start | bytes 65536 | tf_op jit(solution)/shard_map/all_to_all | solution.py:17
  152.0 184.8 %all-reduce.3.cloned.1.call-start = ((), (), s32[]{:S(2)}) async-start(), calls=%async_computation.4 | async-start | bytes 5242880 | tf_op jit(solution)/shard_map/psum | solution.py:137
  159.4 14.2 %copy-start.15 = (bf16[8192,256]{0,1:T(8,128)(2,1)S(1)}, bf16[8192,256]{0,1:T(8,128)(2,1)}, u32[]{:S(2)}) copy-start(bf16[8192,256]{0,1:T(8,128)(2,1)} %all-gather.5.cloned.1.call-done) | copy-start | bytes 12582916
  173.6 5.7 %copy-start.5 = (f32[1024,512]{1,0:T(8,128)S(1)}, f32[1024,512]{1,0:T(8,128)}, u32[]{:S(2)}) copy-start(f32[1024,512]{1,0:T(8,128)} %copy-done.4) | copy-start | bytes 6291460
  173.6 5.7 %copy-start.12 = (bf16[512,256]{1,0:T(8,128)(2,1)S(1)}, bf16[512,256]{1,0:T(8,128)(2,1)}, u32[]{:S(2)}) copy-start(bf16[512,256]{1,0:T(8,128)(2,1)} %param.15) | copy-start | bytes 786436
  179.3 4.4 %copy-start.7 = (bf16[1024,256]{0,1:T(8,128)(2,1)S(1)}, bf16[1024,256]{0,1:T(8,128)(2,1)}, u32[]{:S(2)}) copy-start(bf16[1024,256]{0,1:T(8,128)(2,1)} %fusion.14) | copy-start | bytes 1572868
  185.0 158.7 %copy-start.1 = (bf16[1024,1024]{1,0:T(8,128)(2,1)S(1)}, bf16[1024,1024]{1,0:T(8,128)(2,1)}, u32[]{:S(2)}) copy-start(bf16[1024,1024]{1,0:T(8,128)(2,1)} %param.8) | copy-start | bytes 6291460
  336.8 4.5 %copy-start.8 = (bf16[1024,512]{0,1:T(8,128)(2,1)S(1)}, bf16[1024,512]{0,1:T(8,128)(2,1)}, u32[]{:S(2)}) copy-start(bf16[1024,512]{0,1:T(8,128)(2,1)} %get-tuple-element.18) | copy-start | bytes 3145732
  336.8 6.1 %copy-start.9 = (bf16[512,256]{1,0:T(8,128)(2,1)S(1)}, bf16[512,256]{1,0:T(8,128)(2,1)}, u32[]{:S(2)}) copy-start(bf16[512,256]{1,0:T(8,128)(2,1)} %get-tuple-element.20) | copy-start | bytes 786436
Sparse Core Ops, SparseCore 0:
  13.4 73.7 all-gather.2
  90.1 69.2 all-gather.4
  185.1 151.6 all-reduce.2
where the time goes:
time: 352 us; the launch traced here: 351 us
  waiting for transfers between devices  123 us (35%)
  blocking collectives  91.1 us (26%)
  matrix products  74.8 us (21%)
  other arithmetic  25.5 us (7%)
  between operations  15.8 us (4%)
  starting transfers between devices  11.8 us (3%)
  local copies, waits for them, and re-layouts  9.18 us (3%)
    psum x1, waiting for transfers between devices, body(): lax.psum(grad_user_first.astype(jnp.bfloat16), ('row', 'col'))  86.5 us
    psum x1, blocking collectives, body(): lax.psum(loss_local.astype(jnp.bfloat16), ('row', 'col'))  64.6 us
    all_gather x1, waiting for transfers between devices, body(): lax.all_gather(offered_thing_vector, 'row', axis=0, tiled=True)  32.1 us
    all_gather x1, blocking collectives, body(): lax.all_gather(affinity_sharpness, 'row', axis=0, tiled=True)  26.5 us
    dot_general x1, matrix products, positive_pair_logit(): jnp.dot(sensitivity_of_affinities, gathered_entries, preferred_element_ty...  20.4 us
    reduce_sum x1, other arithmetic, positive_pair_logit(): picked = jnp.sum(jnp.where(target_column, affinity_matrix, 0.0), axis=1)  18.4 us
    dot_general x1, matrix products, positive_pair_logit(): jnp.einsum('ue,ie->ui', shopper_vector, gathered_entries, preferred_eleme...  16 us
    dot_general x1, matrix products, body(): jnp.einsum('ue,ie->ui', all_users, offered_thing_vector, preferred_elemen...  14.2 us
  transfers between devices with their start and end apart: 5, of which 3 were waited for; matrix products, arithmetic and copies ran while one was open for 20% of the time, Pallas kernels for 0%

commit v1 on v0

--- a/solution.py
+++ b/solution.py
@@ -138,7 +138,7 @@
         lax.psum(grad_user_second.astype(jnp.bfloat16), ("row", "col")).astype(jnp.float32),
         lax.psum(grad_item_first.astype(jnp.bfloat16), ("row", "col")).astype(jnp.float32),
         lax.psum(grad_item_second.astype(jnp.bfloat16), ("row", "col")).astype(jnp.float32),
-        lax.psum(loss_local.astype(jnp.bfloat16), ("row", "col")).astype(jnp.float32),
+        lax.psum(lax.psum(loss_local.astype(jnp.bfloat16), "row"), "col").astype(jnp.float32),
     )
     users_total = resident_table * lax.axis_size("row") * lax.axis_size("col")
     return (summed[4] / users_total, summed[0], summed[1], summed[2], summed[3])

time: 352 us -> 352 us (level)
  waiting for transfers between devices: 123 us -> 138 us
  blocking collectives: 91.1 us -> 76.4 us
    psum x1 -> x2, blocking collectives: 64.6 us -> 49.8 us  [the longest x1 33.1 us: body(): lax.psum(lax.psum(loss_local.astype(jnp.bfloat16), 'row'), 'col')]
    psum x1, waiting for transfers between devices: 86.5 us -> 101 us  [body(): lax.psum(grad_user_first.astype(jnp.bfloat16), ('row', 'col'))]
where the time goes in v1:
time: 352 us; the launch traced here: 351 us
  waiting for transfers between devices  138 us (39%)
  blocking collectives  76.4 us (22%)
  matrix products  74.8 us (21%)
  other arithmetic  25.5 us (7%)
  between operations  15.8 us (4%)
  starting transfers between devices  11.8 us (3%)
  local copies, waits for them, and re-layouts  9.17 us (3%)
    psum x1, waiting for transfers between devices, body(): lax.psum(grad_user_first.astype(jnp.bfloat16), ('row', 'col'))  101 us
    psum x1, blocking collectives, body(): lax.psum(lax.psum(loss_local.astype(jnp.bfloat16), 'row'), 'col')  33.1 us
    all_gather x1, waiting for transfers between devices, body(): lax.all_gather(offered_thing_vector, 'row', axis=0, tiled=True)  32.1 us
    all_gather x1, blocking collectives, body(): lax.all_gather(affinity_sharpness, 'row', axis=0, tiled=True)  26.5 us
    dot_general x1, matrix products, positive_pair_logit(): jnp.dot(sensitivity_of_affinities, gathered_entries, preferred_element_ty...  20.4 us
    reduce_sum x1, other arithmetic, positive_pair_logit(): picked = jnp.sum(jnp.where(target_column, affinity_matrix, 0.0), axis=1)  18.4 us
    psum x1, blocking collectives, body(): lax.psum(loss_local.astype(jnp.bfloat16), 'row')  16.7 us
    dot_general x1, matrix products, positive_pair_logit(): jnp.einsum('ue,ie->ui', shopper_vector, gathered_entries, preferred_eleme...  16 us
  transfers between devices with their start and end apart: 5, of which 3 were waited for; matrix products, arithmetic and copies ran while one was open for 20% of the time, Pallas kernels for 0%

profile of v1, /device:TPU:1, one launch (start us, length us, event | category | flops | bytes accessed | tf_op | source)
XLA Modules:
  0.0 351.2 jit_solution(807247302100139430)
XLA Ops:
  7.2 0.0 copy-start
  7.2 0.0 copy-start.11
  7.2 0.0 all-gather.3.cloned.1.call-start
  7.2 3.3 fusion.28
  10.5 0.0 copy-start.4
  10.5 1.3 copy-done.4
  11.8 0.0 copy-done.11
  11.8 0.5 multiply_reduce_fusion
  12.4 0.9 multiply_convert_fusion.8
  13.3 0.0 all-gather.3.cloned.1.call-update
  13.3 0.0 copy-done.14
  13.3 0.6 broadcast_in_dim.15
  13.9 8.3 %all-to-all-start.1 = ((s32[8,1,1024]{2,1,0:T(1,128)}), s32[8,1,1024]{2,1,0:T(1,128)S(1)}, u32[]{:S(2)}, u32[]{:S(2)}) async-start(s32[8,1,1024]{2,1,0:T(1,128)} %broadcast_in_dim.15), calls=%async_computation.1 | async-start | bytes 65536 | tf_op jit(solution)/shard_map/all_to_all | solution.py:17
  22.2 0.0 all-gather.5.cloned.1.call-start
  22.3 0.0 copy-done
  22.3 2.5 fusion.27
  24.8 0.0 copy-start.6
  24.8 1.3 copy-done.6
  26.1 0.0 copy-done.10
  26.1 0.5 multiply_reduce_fusion.1
  26.6 0.0 copy-start.2
  26.6 0.9 copy-done.2
  27.6 0.9 multiply_convert_fusion.9
  28.5 0.0 all-gather.5.cloned.1.call-update
  28.5 0.0 copy-done.13
  28.5 26.5 %all_gather.10 = bf16[8192]{0:T(1024)(128)(2,1)S(1)} all-gather(bf16[1024]{0:T(1024)(128)(2,1)S(1)} %copy-done.13), channel_id=1, replica_groups=mesh['row'=8,'col'=16] {'row'}, dimensions={0}, use_global_device_ids=true | all-gather | bytes 18432 | tf_op jit(solution)/shard_map/all_gather | solution.py:101
  55.1 32.1 %all-gather.3.cloned.1.call-done = bf16[8192,256]{0,1:T(8,128)(2,1)} async-done(((bf16[1024,256]{0,1:T(8,128)(2,1)}), bf16[8192,256]{0,1:T(8,128)(2,1)}) %all-gather.3.cloned.1.call-update) | async-done | bytes 4194320 | tf_op jit(solution)/shard_map/all_gather | solution.py:91
  87.2 16.0 %fusion = (f32[1024]{0:T(1024)S(1)}, f32[1024,8192]{1,0:T(8,128)}) fusion(f32[1024]{0:T(1024)S(1)} %convert_element_type.90, bf16[1024,256]{0,1:T(8,128)(2,1)} %multiply_convert_fusion.9, bf16[8192,256]{0,1:T(8,128)(2,1)} %all-gather.3.cloned.1.call-done), kind=kOutput, calls=%fused_computation.6 | convolution fusion | flops 4320132096 | bytes 38281216 | tf_op jit(solution)/shard_map/ue,ie->ui/dot_general | solution.py:53
  103.2 18.4 %select_reduce_fusion = (f32[1024]{0:T(1024)S(1)}, f32[1024]{0:T(1024)S(1)}) fusion(f32[1024,8192]{1,0:T(8,128)} %get-tuple-element.28, s32[1024]{0:T(1024)S(1)} %copy-done.14, f32[1024]{0:T(1024)S(1)} %convert_element_type.90, f32[1024]{0:T(1024)S(1)} %is-finite_select_fusion), kind=kLoop, calls=%fused_computation.2 | loop fusion | flops 58718208 | bytes 33574912 | tf_op jit(solution)/shard_map/reduce_sum | solution.py:61
  121.6 0.6 subtract_reduce_fusion
  122.2 0.0 copy-done.3
  122.2 20.4 %fusion.9 = (f32[1024]{0:T(1024)S(1)}, bf16[1024,256]{0,1:T(8,128)(2,1)S(1)}) fusion(f32[1024,256]{0,1:T(8,128)S(1)} %copy-done.3, f32[1024]{0:T(1024)S(1)} %add_rsqrt_fusion.1, bf16[8192,256]{0,1:T(8,128)(2,1)} %all-gather.3.cloned.1.call-done, f32[1024,8192]{1,0:T(8,128)} %get-tuple-element.28, f32[1024]{0:T(1024)S(1)} %broadcast_multiply_fusion.1, ...), kind=kOutput, calls=%fused_computation.26 | convolution fusion | flops 4363385856 | bytes 39346176 | tf_op jit(solution)/shard_map/dot_general | solution.py:67
  142.6 1.0 fusion.11
  143.6 4.4 %fusion.5 = bf16[1024,512]{0,1:T(8,128)(2,1)} fusion(bf16[1024,1024]{1,0:T(8,128)(2,1)S(1)} %copy-done, f32[1024,512]{1,0:T(8,128)} %copy-done.6, bf16[1024,256]{0,1:T(8,128)(2,1)} %fusion.11, bf16[512,256]{1,0:T(8,128)(2,1)S(1)} %copy-done.10), kind=kOutput, calls=%fused_computation.16 | convolution fusion | flops 1344274432 | bytes 6029312 | tf_op jit(solution)/shard_map/dot_general | solution.py:42
  148.0 0.0 all-to-all-done.1
  148.0 0.6 broadcast_in_dim.14
  148.6 3.3 all-to-all-start
  152.0 0.0 all-reduce.3.cloned.1.call-start
  152.0 2.9 convolution_convert_fusion.3
  154.9 4.5 %all-gather.5.cloned.1.call-done = bf16[8192,256]{0,1:T(8,128)(2,1)} async-done(((bf16[1024,256]{0,1:T(8,128)(2,1)}), bf16[8192,256]{0,1:T(8,128)(2,1)}) %all-gather.5.cloned.1.call-update) | async-done | bytes 4194320 | tf_op jit(solution)/shard_map/all_gather | solution.py:100
  159.4 0.0 all-to-all-done
  159.4 14.2 %multiply_convert_fusion.5.clone.4 = bf16[8192,1024]{1,0:T(8,128)(2,1)S(1)} fusion(f32[8192]{0:T(1024)S(1)} %broadcast_multiply_fusion, s32[1024]{0:T(1024)S(1)} %iota_add_fusion, f32[8192]{0:T(1024)S(1)} %bitcast.31, f32[8192]{0:T(1024)S(1)} %convert_element_type.108, s32[8192]{0:T(1024)S(1)} %bitcast.30, ...), kind=kOutput, calls=%fused_computation.clone.clone.clone.clone.clone.clone.1 | convolution fusion | flops 4362600448 | bytes 22159360 | tf_op jit(solution)/shard_map/ue,ie->ui/dot_general | solution.py:108
  173.6 0.0 copy-done.15
  173.6 0.0 copy-start.5
  173.6 0.0 copy-start.12
  173.7 4.7 %fusion.12 = (f32[1024]{0:T(1024)S(1)}, bf16[1024,256]{0,1:T(8,128)(2,1)S(1)}) fusion(f32[1024,256]{0,1:T(8,128)S(1)} %get-tuple-element.26, f32[1024]{0:T(1024)S(1)} %add_rsqrt_fusion, bf16[8192,256]{0,1:T(8,128)(2,1)S(1)} %copy-done.15, bf16[8192,1024]{1,0:T(8,128)(2,1)S(1)} %multiply_convert_fusion.5.clone.4), kind=kOutput, calls=%fused_computation.29 | convolution fusion | flops 4296276992 | bytes 22552576 | tf_op jit(solution)/shard_map/ui,ue->ie/dot_general | solution.py:121
  178.3 1.0 fusion.14
  179.3 0.0 copy-done.5
  179.3 0.0 copy-done.12
  179.3 4.4 %fusion.6 = bf16[1024,512]{0,1:T(8,128)(2,1)} fusion(bf16[1024,1024]{1,0:T(8,128)(2,1)} %param.9, f32[1024,512]{1,0:T(8,128)S(1)} %copy-done.5, bf16[1024,256]{0,1:T(8,128)(2,1)} %fusion.14, bf16[512,256]{1,0:T(8,128)(2,1)S(1)} %copy-done.12), kind=kOutput, calls=%fused_computation.17 | convolution fusion | flops 1344274432 | bytes 6029312 | tf_op jit(solution)/shard_map/dot_general | solution.py:42
  183.7 0.0 copy-done.7
  183.7 1.2 convolution_convert_fusion.2
  184.9 0.0 all-reduce.3.cloned.1.call-update
  185.0 0.0 copy-start.1
  185.0 16.7 %psum.42 = bf16[]{:T(256)} all-reduce(bf16[]{:T(256)} %get-tuple-element.21), channel_id=1, replica_groups=mesh['row'=8,'col'=16] {'row'}, use_global_device_ids=true, to_apply=%region_6.7 | all-reduce | flops 1 | bytes 4 | tf_op jit(solution)/shard_map/psum | solution.py:141
  201.7 33.1 %psum.43 = bf16[]{:T(256)} all-reduce(bf16[]{:T(256)} %psum.42), channel_id=1, replica_groups=mesh['row'=8,'col'=16] {'col'}, use_global_device_ids=true, to_apply=%region_7.8 | all-reduce | flops 1 | bytes 4 | tf_op jit(solution)/shard_map/psum | solution.py:141
  235.5 101.1 %all-reduce.3.cloned.1.call-done = (bf16[1024,512]{0,1:T(8,128)(2,1)}, bf16[1024,512]{0,1:T(8,128)(2,1)}, bf16[512,256]{1,0:T(8,128)(2,1)}, bf16[512,256]{1,0:T(8,128)(2,1)}) async-done(((bf16[1024,512]{0,1:T(8,128)(2,1)}, bf16[1024,512]{0,1:T(8,128)(2,1)}, bf16[512,256]{1,0:T(8,128)(2,1)}, bf16[512,256]{1,0:T(8,128)(2,1)}), (bf16[1024,512]{0,1:T(8,128)(2,1)}, bf16[1024,512]{0,1:T(8,128)(2,1)}, ...) | async-done | bytes 2621456 | tf_op jit(solution)/shard_map/psum | solution.py:137
  336.6 2.7 copy.15
  339.3 1.8 convert_element_type.107
  341.1 0.0 copy-done.8
  341.1 1.6 copy.16
  342.7 0.0 copy-done.9
  342.7 0.8 convert_element_type.119
  343.5 0.0 copy-done.1
  (18 shorter events, 0.1 us)
Async XLA Ops:
  7.2 15.1 %copy-start = (bf16[1024,1024]{1,0:T(8,128)(2,1)S(1)}, bf16[1024,1024]{1,0:T(8,128)(2,1)}, u32[]{:S(2)}) copy-start(bf16[1024,1024]{1,0:T(8,128)(2,1)} %param.8) | copy-start | bytes 6291460
  7.2 4.7 %copy-start.11 = (bf16[512,256]{1,0:T(8,128)(2,1)S(1)}, bf16[512,256]{1,0:T(8,128)(2,1)}, u32[]{:S(2)}) copy-start(bf16[512,256]{1,0:T(8,128)(2,1)} %param.15) | copy-start | bytes 786436
  7.2 80.0 %all-gather.3.cloned.1.call-start = ((), (), s32[]{:S(2)}) async-start(), calls=%async_computation.2 | async-start | bytes 4718592 | tf_op jit(solution)/shard_map/all_gather | solution.py:91
  10.5 1.3 copy-start.4
  11.8 1.4 copy-start.14
  13.9 134.1 %all-to-all-start.1 = ((s32[8,1,1024]{2,1,0:T(1,128)}), s32[8,1,1024]{2,1,0:T(1,128)S(1)}, u32[]{:S(2)}, u32[]{:S(2)}) async-start(s32[8,1,1024]{2,1,0:T(1,128)} %broadcast_in_dim.15), calls=%async_computation.1 | async-start | bytes 65536 | tf_op jit(solution)/shard_map/all_to_all | solution.py:17
  22.2 3.9 %copy-start.10 = (bf16[512,256]{1,0:T(8,128)(2,1)S(1)}, bf16[512,256]{1,0:T(8,128)(2,1)}, u32[]{:S(2)}) copy-start(bf16[512,256]{1,0:T(8,128)(2,1)} %param.13) | copy-start | bytes 786436
  22.2 137.2 %all-gather.5.cloned.1.call-start = ((), (), s32[]{:S(2)}) async-start(), calls=%async_computation.3 | async-start | bytes 4718592 | tf_op jit(solution)/shard_map/all_gather | solution.py:100
  24.8 1.3 copy-start.6
  26.1 2.4 copy-start.13
  26.6 1.0 copy-start.2
  103.2 19.0 %copy-start.3 = (f32[1024,256]{0,1:T(8,128)S(1)}, f32[1024,256]{0,1:T(8,128)}, u32[]{:S(2)}) copy-start(f32[1024,256]{0,1:T(8,128)} %copy-done.2) | copy-start | bytes 3145732
  148.6 10.8 %all-to-all-start = ((f32[8,1,1024]{2,1,0:T(1,128)}), f32[8,1,1024]{2,1,0:T(1,128)S(1)}, u32[]{:S(2)}, u32[]{:S(2)}) async-start(f32[8,1,1024]{2,1,0:T(1,128)} %broadcast_in_dim.14), calls=%async_computation | async-start | bytes 65536 | tf_op jit(solution)/shard_map/all_to_all | solution.py:17
  152.0 184.7 %all-reduce.3.cloned.1.call-start = ((), (), s32[]{:S(2)}) async-start(), calls=%async_computation.4 | async-start | bytes 5242880 | tf_op jit(solution)/shard_map/psum | solution.py:137
  159.4 14.2 %copy-start.15 = (bf16[8192,256]{0,1:T(8,128)(2,1)S(1)}, bf16[8192,256]{0,1:T(8,128)(2,1)}, u32[]{:S(2)}) copy-start(bf16[8192,256]{0,1:T(8,128)(2,1)} %all-gather.5.cloned.1.call-done) | copy-start | bytes 12582916
  173.6 5.7 %copy-start.5 = (f32[1024,512]{1,0:T(8,128)S(1)}, f32[1024,512]{1,0:T(8,128)}, u32[]{:S(2)}) copy-start(f32[1024,512]{1,0:T(8,128)} %copy-done.4) | copy-start | bytes 6291460
  173.6 5.7 %copy-start.12 = (bf16[512,256]{1,0:T(8,128)(2,1)S(1)}, bf16[512,256]{1,0:T(8,128)(2,1)}, u32[]{:S(2)}) copy-start(bf16[512,256]{1,0:T(8,128)(2,1)} %param.15) | copy-start | bytes 786436
  179.3 4.4 %copy-start.7 = (bf16[1024,256]{0,1:T(8,128)(2,1)S(1)}, bf16[1024,256]{0,1:T(8,128)(2,1)}, u32[]{:S(2)}) copy-start(bf16[1024,256]{0,1:T(8,128)(2,1)} %fusion.14) | copy-start | bytes 1572868
  185.0 158.6 %copy-start.1 = (bf16[1024,1024]{1,0:T(8,128)(2,1)S(1)}, bf16[1024,1024]{1,0:T(8,128)(2,1)}, u32[]{:S(2)}) copy-start(bf16[1024,1024]{1,0:T(8,128)(2,1)} %param.8) | copy-start | bytes 6291460
  336.6 4.5 %copy-start.8 = (bf16[1024,512]{0,1:T(8,128)(2,1)S(1)}, bf16[1024,512]{0,1:T(8,128)(2,1)}, u32[]{:S(2)}) copy-start(bf16[1024,512]{0,1:T(8,128)(2,1)} %get-tuple-element.18) | copy-start | bytes 3145732
  336.6 6.1 %copy-start.9 = (bf16[512,256]{1,0:T(8,128)(2,1)S(1)}, bf16[512,256]{1,0:T(8,128)(2,1)}, u32[]{:S(2)}) copy-start(bf16[512,256]{1,0:T(8,128)(2,1)} %get-tuple-element.20) | copy-start | bytes 786436
Sparse Core Ops, SparseCore 0:
  13.4 73.7 all-gather.2
  90.1 69.2 all-gather.4
  185.1 151.4 all-reduce.2
